TPU v7x, 128 devices: a whole 4x4x4 slice. The times are simulated.
128 devices in a mesh: row: 8 (over x_hi, z), col: 8 (over y, x_lo), layer: 2 (over core).
Axes of the slice: x: 4 (x_hi: 2, x_lo: 2; x = x_hi * 2 + x_lo), y: 4, z: 4, core: 2. Of those that a mesh axis runs over, the one named last changes fastest.
Arguments:
- expression: bfloat16 [24576, 1024], P(('row', 'col'), 'layer'), may hold values from -240 to 240
Outputs:
- connectivity: float32 [24576], P(('row', 'col', 'layer'))
All inputs are finite; a program needn't handle non-finite values.
Results may differ from a plain program's by a relative error of at most 0.00048.
Values may be sent and summed in bfloat16 or wider, within the bound.
No kernel may reach another device: no remote copies, remote signals or barrier semaphores. Data moves between devices by JAX's collectives and lax.ppermute only.
A program may use at most 64 MiB of HBM per device.

v0:
```python
import jax
import jax.numpy as jnp
from jax import lax
from jax.sharding import Mesh
from jax.sharding import PartitionSpec as P

S = 1024
COL = ("col_0", "col_1")
COL_LAYER = ("col_0", "col_1", "layer")
ROW_COL = ("row", "col_0", "col_1")
ROW_COL_LAYER = ("row", "col_0", "col_1", "layer")
epsilon = 1e-05


def whole_of(value, axes, dim):
    whole = value
    for number in range(len(axes) - 1, -1, -1):
        whole = lax.all_gather(whole, axes[number], axis=dim, tiled=True)
    return whole


def cut_along(value, dim, length):
    before, after = (value.shape[:dim], value.shape[dim + 1 :])
    return jnp.moveaxis(value.reshape(*before, length, -1, *after), dim, 0)


def sum_at_owner(value, axis, dim):
    length = lax.axis_size(axis)
    blocks = lax.all_to_all(cut_along(value, dim, length), axis, 0, 0, tiled=True)
    return jnp.sum(blocks, axis=0)


def adjacency(correlation):
    shifted = (1.0 + correlation) * 0.5
    square = shifted * shifted
    fourth = square * square
    eighth = fourth * fourth
    return eighth * fourth


def standardize(values, total, squares):
    average = total / S
    variance = squares / S - average * average
    return ((values - average[:, None]) * lax.rsqrt(variance + epsilon)[:, None]).astype(
        jnp.bfloat16
    )


def pair_products(left, right):
    return lax.dot_general(
        left, right, (((1,), (1,)), ((), ())), preferred_element_type=jnp.float32
    )


def on_device(expression):
    whole = lax.all_gather(expression, "layer", axis=1, tiled=True)
    values = whole.astype(jnp.float32)
    scaled = standardize(values, jnp.sum(values, axis=1), jnp.sum(values * values, axis=1))
    row_genes = whole_of(scaled, COL, 0)
    share = scaled.shape[0] // lax.axis_size("layer")
    own_half = lax.dynamic_slice_in_dim(scaled, lax.axis_index("layer") * share, share, 0)
    partial_value = jnp.sum(
        adjacency(
            pair_products(lax.all_gather(own_half, "row", axis=0, tiled=True), row_genes) / S
        ),
        axis=0,
    )
    summed = sum_at_owner(partial_value, COL_LAYER, 0)
    return summed - 1.0


def solution(mesh):
    torus = Mesh(
        mesh.devices.reshape(mesh.shape["row"], 4, 2, mesh.shape["layer"]),
        ("row", "col_0", "col_1", "layer"),
    )
    in_specs = (P(ROW_COL, "layer"),)
    out_specs = P(ROW_COL_LAYER)
    return jax.shard_map(
        on_device, mesh=torus, in_specs=in_specs, out_specs=out_specs, check_vma=False
    )
```

profile of v0, /device:TPU:1, one launch (start us, length us, event | category | flops | bytes accessed | tf_op | source)
XLA Modules:
  0.0 208.2 jit_solution(15841758606640467007)
XLA Ops:
  6.5 0.0 all-gather.6.cloned.1.call-start
  6.5 3.6 %all_gather.12 = bf16[384,1024]{1,0:T(8,128)(2,1)S(1)} all-gather(bf16[384,512]{1,0:T(8,128)(2,1)} %param.1), channel_id=1, replica_groups=mesh['row'=8,'col_0'=4,'col_1'=2,'layer'=2] {'layer'}, dimensions={1}, use_global_device_ids=true | all-gather | bytes 1179648 | tf_op jit(solution)/shard_map/all_gather | solution.py:56
  10.1 0.3 convert_reduce_fusion
  10.4 1.1 fusion.2
  11.6 0.0 all-gather.6.cloned.1.call-update
  11.6 0.0 all-gather.4.cloned.1.call-start
  11.7 1.8 constant_dynamic-slice_fusion
  13.4 0.0 all-gather.4.cloned.1.call-update
  13.5 0.0 all-gather.8.cloned.1.call-start
  13.5 30.0 %all-gather.6.cloned.1.call-done = bf16[768,1024]{1,0:T(8,128)(2,1)} async-done(((bf16[384,1024]{1,0:T(8,128)(2,1)}), bf16[768,1024]{1,0:T(8,128)(2,1)}) %all-gather.6.cloned.1.call-update) | async-done | bytes 1572880 | tf_op jit(solution)/shard_map/all_gather | solution.py:18
  43.5 0.0 all-gather.8.cloned.1.call-update
  43.5 65.1 %all-gather.4.cloned.1.call-done = bf16[1536,1024]{1,0:T(8,128)(2,1)} async-done(((bf16[192,1024]{1,0:T(8,128)(2,1)}), bf16[1536,1024]{1,0:T(8,128)(2,1)}) %all-gather.4.cloned.1.call-update) | async-done | bytes 3145744 | tf_op jit(solution)/shard_map/all_gather | solution.py:64
  108.6 65.7 %all-gather.8.cloned.1.call-done = bf16[3072,1024]{1,0:T(8,128)(2,1)} async-done(((bf16[768,1024]{1,0:T(8,128)(2,1)}), bf16[3072,1024]{1,0:T(8,128)(2,1)}) %all-gather.8.cloned.1.call-update) | async-done | bytes 6291472 | tf_op jit(solution)/shard_map/all_gather | solution.py:18
  174.3 15.7 %fusion = f32[3072]{0:T(1024)S(1)} fusion(bf16[1536,1024]{1,0:T(8,128)(2,1)} %all-gather.4.cloned.1.call-done, bf16[3072,1024]{1,0:T(8,128)(2,1)} %all-gather.8.cloned.1.call-done), kind=kOutput, calls=%fused_computation.1 | convolution fusion | flops 9701422080 | bytes 9449472 | tf_op jit(solution)/shard_map/dot_general | solution.py:50
  190.0 0.1 all_to_all.6
  190.1 11.0 %all_to_all.9 = f32[16,1,192]{2,1,0:T(1,128)S(1)} all-to-all(f32[16,1,192]{2,1,0:T(1,128)S(1)} %all_to_all.6), channel_id=1, replica_groups=mesh['row'=8,'col_0'=4,'col_1'=2,'layer'=2] {'col_0','col_1','layer'}, dimensions={0} | all-to-all | bytes 24576 | tf_op jit(solution)/shard_map/all_to_all | solution.py:29
  201.1 0.6 broadcast_add_fusion
  (2 shorter events, 0.0 us)
Async XLA Ops:
  6.5 36.9 %all-gather.6.cloned.1.call-start = ((), (), s32[]{:S(2)}) async-start(), calls=%async_computation.2 | async-start | bytes 2359296 | tf_op jit(solution)/shard_map/all_gather | solution.py:18
  11.6 97.0 %all-gather.4.cloned.1.call-start = ((), (), s32[]{:S(2)}) async-start(), calls=%async_computation.1 | async-start | bytes 3538944 | tf_op jit(solution)/shard_map/all_gather | solution.py:64
  13.5 160.9 %all-gather.8.cloned.1.call-start = ((), (), s32[]{:S(2)}) async-start(), calls=%async_computation.3 | async-start | bytes 7864320 | tf_op jit(solution)/shard_map/all_gather | solution.py:18
Sparse Core Ops, SparseCore 0:
  11.7 31.7 all-gather.5
  45.8 62.8 all-gather.3
  110.3 63.9 all-gather.7
where the time goes:
time: 208 us
  waiting for transfers between devices  161 us (77%)
  matrix products  15.7 us (8%)
  blocking collectives  14.6 us (7%)
  between operations  13.1 us (6%)
    all_gather x2, waiting for transfers between devices, whole_of(): whole = lax.all_gather(whole, axes[number], axis=dim, tiled=True)  95.6 us
    all_gather x1, waiting for transfers between devices, on_device(): lax.all_gather(own_half, 'row', axis=0, tiled=True)  65.1 us
    dot_general x1, matrix products, pair_products(): lax.dot_general(left, right, (((1,), (1,)), ((), ())), preferred_element_...  15.7 us
    all_to_all x1, blocking collectives, sum_at_owner(): lax.all_to_all(cut_along(value, dim, length), axis, 0, 0, tiled=True)  11 us
  transfers between devices with their start and end apart: 3, of which 3 were waited for; matrix products, arithmetic and copies ran while one was open for 1% of the time, Pallas kernels for 0%

commit v1 on v0

--- a/solution.py
+++ b/solution.py
@@ -61,7 +61,14 @@
     own_half = lax.dynamic_slice_in_dim(scaled, lax.axis_index("layer") * share, share, 0)
     partial_value = jnp.sum(
         adjacency(
-            pair_products(lax.all_gather(own_half, "row", axis=0, tiled=True), row_genes) / S
+            pair_products(
+                jnp.concatenate(
+                    lax.all_to_all(jnp.stack([own_half] * lax.axis_size("row")), "row", 0, 0),
+                    axis=0,
+                ),
+                row_genes,
+            )
+            / S
         ),
         axis=0,
     )

time: 208 us -> 145 us (0.70)
  waiting for transfers between devices: 161 us -> 54.7 us
  blocking collectives: 14.6 us -> 58.6 us
    all_gather x1 -> x0, waiting for transfers between devices: 65.1 us -> none  [on_device(): lax.all_gather(own_half, 'row', axis=0, tiled=True)]
    all_to_all x0 -> x1, blocking collectives: none -> 44 us  [on_device(): lax.all_to_all(jnp.stack([own_half] * lax.axis_size('row')), 'row', 0, 0)]
    all_gather x2, waiting for transfers between devices: 95.6 us -> 54.7 us  [whole_of(): whole = lax.all_gather(whole, axes[number], axis=dim, tiled=True)]
  transfers between devices with their start and end apart: 3 -> 2, of which waited for: 3 -> 2; matrix products, arithmetic and copies ran while one was open for 1% -> 1% of each run, Pallas kernels for 0% -> 0%
where the time goes in v1:
time: 145 us
  blocking collectives  58.6 us (40%)
  waiting for transfers between devices  54.7 us (38%)
  matrix products  14.7 us (10%)
  between operations  13.4 us (9%)
  other arithmetic  2.12 us (1%)
  local copies, waits for them, and re-layouts  1.5 us (1%)
    all_gather x2, waiting for transfers between devices, whole_of(): whole = lax.all_gather(whole, axes[number], axis=dim, tiled=True)  54.7 us
    all_to_all x1, blocking collectives, on_device(): lax.all_to_all(jnp.stack([own_half] * lax.axis_size('row')), 'row', 0, 0)  44 us
    dot_general x1, matrix products, pair_products(): lax.dot_general(left, right, (((1,), (1,)), ((), ())), preferred_element_...  14.7 us
    all_to_all x1, blocking collectives, sum_at_owner(): lax.all_to_all(cut_along(value, dim, length), axis, 0, 0, tiled=True)  11 us
    all_gather x1, blocking collectives, on_device(): whole = lax.all_gather(expression, 'layer', axis=1, tiled=True)  3.58 us
  transfers between devices with their start and end apart: 2, of which 2 were waited for; matrix products, arithmetic and copies ran while one was open for 1% of the time, Pallas kernels for 0%

profile of v1, /device:TPU:1, one launch (start us, length us, event | category | flops | bytes accessed | tf_op | source)
XLA Modules:
  0.0 145.1 jit_solution(4109163026546437779)
XLA Ops:
  6.5 0.0 all-gather.3.cloned.1.call-start
  6.5 3.6 %all_gather.9 = bf16[384,1024]{1,0:T(8,128)(2,1)S(1)} all-gather(bf16[384,512]{1,0:T(8,128)(2,1)} %param.1), channel_id=1, replica_groups=mesh['row'=8,'col_0'=4,'col_1'=2,'layer'=2] {'layer'}, dimensions={1}, use_global_device_ids=true | all-gather | bytes 1179648 | tf_op jit(solution)/shard_map/all_gather | solution.py:56
  10.1 0.3 convert_reduce_fusion
  10.4 1.2 fusion.2
  11.6 0.0 all-gather.3.cloned.1.call-update
  11.7 0.0 all-gather.5.cloned.1.call-start
  11.7 31.8 %all-gather.3.cloned.1.call-done = bf16[768,1024]{1,0:T(8,128)(2,1)} async-done(((bf16[384,1024]{1,0:T(8,128)(2,1)}), bf16[768,1024]{1,0:T(8,128)(2,1)}) %all-gather.3.cloned.1.call-update) | async-done | bytes 1572880 | tf_op jit(solution)/shard_map/all_gather | solution.py:18
  43.5 0.0 all-gather.5.cloned.1.call-update
  43.6 1.0 constant_dynamic-slice_fusion
  44.6 0.4 stack.2
  45.0 44.0 %all_to_all.14 = bf16[8,192,1024]{2,1,0:T(8,128)(2,1)S(1)} all-to-all(bf16[8,192,1024]{2,1,0:T(8,128)(2,1)S(1)} %stack.2), channel_id=1, replica_groups=mesh['row'=8,'col_0'=4,'col_1'=2,'layer'=2] {'row'}, dimensions={0} | all-to-all | bytes 6291456 | tf_op jit(solution)/shard_map/all_to_all | solution.py:66
  89.0 22.9 %all-gather.5.cloned.1.call-done = bf16[3072,1024]{1,0:T(8,128)(2,1)} async-done(((bf16[768,1024]{1,0:T(8,128)(2,1)}), bf16[3072,1024]{1,0:T(8,128)(2,1)}) %all-gather.5.cloned.1.call-update) | async-done | bytes 6291472 | tf_op jit(solution)/shard_map/all_gather | solution.py:18
  111.9 14.7 %fusion = f32[3072]{0:T(1024)S(1)} fusion(bf16[1536,1024]{1,0:T(8,128)(2,1)S(1)} %bitcast.3, bf16[3072,1024]{1,0:T(8,128)(2,1)} %all-gather.5.cloned.1.call-done), kind=kOutput, calls=%fused_computation.1 | convolution fusion | flops 9701422080 | bytes 9449472 | tf_op jit(solution)/shard_map/dot_general | solution.py:50
  126.6 0.1 all_to_all.10
  126.7 11.0 %all_to_all.15 = f32[16,1,192]{2,1,0:T(1,128)S(1)} all-to-all(f32[16,1,192]{2,1,0:T(1,128)S(1)} %all_to_all.10), channel_id=1, replica_groups=mesh['row'=8,'col_0'=4,'col_1'=2,'layer'=2] {'col_0','col_1','layer'}, dimensions={0} | all-to-all | bytes 24576 | tf_op jit(solution)/shard_map/all_to_all | solution.py:29
  137.7 0.6 broadcast_add_fusion
  (2 shorter events, 0.0 us)
Async XLA Ops:
  6.5 37.0 %all-gather.3.cloned.1.call-start = ((), (), s32[]{:S(2)}) async-start(), calls=%async_computation.2 | async-start | bytes 2359296 | tf_op jit(solution)/shard_map/all_gather | solution.py:18
  11.7 100.2 %all-gather.5.cloned.1.call-start = ((), (), s32[]{:S(2)}) async-start(), calls=%async_computation.3 | async-start | bytes 7864320 | tf_op jit(solution)/shard_map/all_gather | solution.py:18
Sparse Core Ops, SparseCore 0:
  11.8 31.7 all-gather.2
  45.2 66.6 all-gather.4
